TPU v7x, 8 devices: a whole 2x2x1 slice. The times are simulated.
8 devices in a mesh: parts: 1 (over z), feat: 2 (over y), data: 4 (over x, core).
Axes of the slice: x: 2, y: 2, z: 1, core: 2. Of those that a mesh axis runs over, the one named last changes fastest.
Arguments:
- x_data: bfloat16 [32768, 4096], P('data', 'feat')
- labels: int32 [32768], P('data')
- theta_init: float32 [4096, 128], P('feat', 'parts')
- mom_init: float32 [4096, 128], P('feat', 'parts')
- step_size: float32 [128], P('parts')
Outputs:
- output 1: float32 [4096, 128], P('feat', 'parts')
- output 2: float32 [4096, 128], P('feat', 'parts')
- output 3: float32 [128], P('parts')
All inputs are finite; a program needn't handle non-finite values.
Results may differ from a plain program's by a relative error of at most 0.001.
Values are sent between devices in bfloat16 or wider.
A program may use at most 1 GiB of HBM per device.

v0:
```python
import jax
import jax.numpy as jnp
from jax import lax
from jax.sharding import PartitionSpec as P

LEAPS = 16
PRIOR_VAR = 4.0


def solution(mesh):
    chain_spec = P("feat", "parts")

    def local_run(x_local, labels, theta_init, mom_init, step_size):
        label_col = labels.astype(jnp.float32)[:, None]

        def gradient_at(position):
            part_logits = jnp.dot(x_local, position.astype(jnp.bfloat16), preferred_element_type=jnp.float32)
            logits = lax.psum(part_logits, "feat")
            residual = (label_col - jax.nn.sigmoid(logits)).astype(jnp.bfloat16)
            local_grad = lax.dot_general(x_local, residual, (((0,), (0,)), ((), ())), preferred_element_type=jnp.float32)
            return lax.psum(local_grad, "data") - position / PRIOR_VAR, logits

        half_step = 0.5 * step_size
        gradient, logits = gradient_at(theta_init)
        momentum = mom_init + half_step * gradient
        position = theta_init
        for unused in range(LEAPS - 1):
            position = position + step_size * momentum
            gradient, logits = gradient_at(position)
            momentum = momentum + step_size * gradient
        position = position + step_size * momentum
        gradient, logits = gradient_at(position)
        momentum = momentum + half_step * gradient
        like_sum = lax.psum(jnp.sum(jax.nn.softplus(logits) - label_col * logits, axis=0), "data")
        norm_sum = lax.psum(jnp.sum(position * position, axis=0) / (2.0 * PRIOR_VAR)
                            + 0.5 * jnp.sum(momentum * momentum, axis=0), "feat")
        return position, momentum, like_sum + norm_sum

    return jax.shard_map(local_run, mesh=mesh,
                         in_specs=(P("data", "feat"), P("data"), chain_spec, chain_spec, P("parts")),
                         out_specs=(chain_spec, chain_spec, P("parts")), check_vma=False)
```

profile of v0, /device:TPU:0, one launch (start us, length us, event | category | flops | bytes accessed | tf_op | source)
XLA Modules:
  0.0 2924.9 jit_solution(8766672405588021388)
XLA Ops:
  7.2 18.0 fusion.52
  25.9 104.3 %all-reduce.35.cloned.1.call-done = f32[8192,128]{0,1:T(8,128)} async-done(((f32[8192,128]{0,1:T(8,128)}), f32[8192,128]{0,1:T(8,128)}) %all-reduce.35.cloned.1.call-update) | async-done | bytes 4194320 | tf_op jit(solution)/shard_map/psum | solution.py:18
  130.2 17.4 convolution_bitcast_fusion.32
  149.7 29.0 all-reduce.37.cloned.1.call-done
  178.7 18.2 convolution_bitcast_fusion.15
  197.1 102.2 %all-reduce.39.cloned.1.call-done = f32[8192,128]{0,1:T(8,128)} async-done(((f32[8192,128]{0,1:T(8,128)}), f32[8192,128]{0,1:T(8,128)}) %all-reduce.39.cloned.1.call-update) | async-done | bytes 4194320 | tf_op jit(solution)/shard_map/psum | solution.py:18
  299.3 17.4 convolution_bitcast_fusion.31
  316.8 30.9 %all-reduce.41.cloned.1.call-done = f32[2048,128]{0,1:T(8,128)} async-done(((f32[2048,128]{0,1:T(8,128)}), f32[2048,128]{0,1:T(8,128)}) %all-reduce.41.cloned.1.call-update) | async-done | bytes 1048592 | tf_op jit(solution)/shard_map/psum | solution.py:21
  349.8 17.4 convolution_bitcast_fusion.14
  367.3 102.4 %all-reduce.43.cloned.1.call-done = f32[8192,128]{0,1:T(8,128)} async-done(((f32[8192,128]{0,1:T(8,128)}), f32[8192,128]{0,1:T(8,128)}) %all-reduce.43.cloned.1.call-update) | async-done | bytes 4194320 | tf_op jit(solution)/shard_map/psum | solution.py:18
  469.7 17.4 convolution_bitcast_fusion.30
  487.6 30.5 %all-reduce.45.cloned.1.call-done = f32[2048,128]{0,1:T(8,128)} async-done(((f32[2048,128]{0,1:T(8,128)}), f32[2048,128]{0,1:T(8,128)}) %all-reduce.45.cloned.1.call-update) | async-done | bytes 1048592 | tf_op jit(solution)/shard_map/psum | solution.py:21
  521.0 17.8 convolution_bitcast_fusion.13
  538.9 102.4 %all-reduce.47.cloned.1.call-done = f32[8192,128]{0,1:T(8,128)} async-done(((f32[8192,128]{0,1:T(8,128)}), f32[8192,128]{0,1:T(8,128)}) %all-reduce.47.cloned.1.call-update) | async-done | bytes 4194320 | tf_op jit(solution)/shard_map/psum | solution.py:18
  641.3 17.4 convolution_bitcast_fusion.29
  658.7 30.9 %all-reduce.49.cloned.1.call-done = f32[2048,128]{0,1:T(8,128)} async-done(((f32[2048,128]{0,1:T(8,128)}), f32[2048,128]{0,1:T(8,128)}) %all-reduce.49.cloned.1.call-update) | async-done | bytes 1048592 | tf_op jit(solution)/shard_map/psum | solution.py:21
  691.3 17.4 convolution_bitcast_fusion.12
  708.9 102.3 %all-reduce.51.cloned.1.call-done = f32[8192,128]{0,1:T(8,128)} async-done(((f32[8192,128]{0,1:T(8,128)}), f32[8192,128]{0,1:T(8,128)}) %all-reduce.51.cloned.1.call-update) | async-done | bytes 4194320 | tf_op jit(solution)/shard_map/psum | solution.py:18
  811.2 17.4 convolution_bitcast_fusion.28
  828.6 30.9 %all-reduce.53.cloned.1.call-done = f32[2048,128]{0,1:T(8,128)} async-done(((f32[2048,128]{0,1:T(8,128)}), f32[2048,128]{0,1:T(8,128)}) %all-reduce.53.cloned.1.call-update) | async-done | bytes 1048592 | tf_op jit(solution)/shard_map/psum | solution.py:21
  861.9 17.4 convolution_bitcast_fusion.11
  879.4 102.4 %all-reduce.55.cloned.1.call-done = f32[8192,128]{0,1:T(8,128)} async-done(((f32[8192,128]{0,1:T(8,128)}), f32[8192,128]{0,1:T(8,128)}) %all-reduce.55.cloned.1.call-update) | async-done | bytes 4194320 | tf_op jit(solution)/shard_map/psum | solution.py:18
  981.8 17.4 convolution_bitcast_fusion.27
  999.5 30.7 %all-reduce.57.cloned.1.call-done = f32[2048,128]{0,1:T(8,128)} async-done(((f32[2048,128]{0,1:T(8,128)}), f32[2048,128]{0,1:T(8,128)}) %all-reduce.57.cloned.1.call-update) | async-done | bytes 1048592 | tf_op jit(solution)/shard_map/psum | solution.py:21
  1031.8 17.4 convolution_bitcast_fusion.10
  1049.3 102.4 %all-reduce.59.cloned.1.call-done = f32[8192,128]{0,1:T(8,128)} async-done(((f32[8192,128]{0,1:T(8,128)}), f32[8192,128]{0,1:T(8,128)}) %all-reduce.59.cloned.1.call-update) | async-done | bytes 4194320 | tf_op jit(solution)/shard_map/psum | solution.py:18
  1151.7 17.4 convolution_bitcast_fusion.26
  1169.2 30.9 %all-reduce.61.cloned.1.call-done = f32[2048,128]{0,1:T(8,128)} async-done(((f32[2048,128]{0,1:T(8,128)}), f32[2048,128]{0,1:T(8,128)}) %all-reduce.61.cloned.1.call-update) | async-done | bytes 1048592 | tf_op jit(solution)/shard_map/psum | solution.py:21
  1203.2 17.4 convolution_bitcast_fusion.9
  1221.1 102.0 %all-reduce.63.cloned.1.call-done = f32[8192,128]{0,1:T(8,128)} async-done(((f32[8192,128]{0,1:T(8,128)}), f32[8192,128]{0,1:T(8,128)}) %all-reduce.63.cloned.1.call-update) | async-done | bytes 4194320 | tf_op jit(solution)/shard_map/psum | solution.py:18
  1323.1 17.4 convolution_bitcast_fusion.25
  1340.6 30.9 %all-reduce.65.cloned.1.call-done = f32[2048,128]{0,1:T(8,128)} async-done(((f32[2048,128]{0,1:T(8,128)}), f32[2048,128]{0,1:T(8,128)}) %all-reduce.65.cloned.1.call-update) | async-done | bytes 1048592 | tf_op jit(solution)/shard_map/psum | solution.py:21
  1390.5 102.4 %all-reduce.67.cloned.1.call-done = f32[8192,128]{0,1:T(8,128)} async-done(((f32[8192,128]{0,1:T(8,128)}), f32[8192,128]{0,1:T(8,128)}) %all-reduce.67.cloned.1.call-update) | async-done | bytes 4194320 | tf_op jit(solution)/shard_map/psum | solution.py:18
  1493.0 17.4 convolution_bitcast_fusion.24
  1510.6 30.8 %all-reduce.69.cloned.1.call-done = f32[2048,128]{0,1:T(8,128)} async-done(((f32[2048,128]{0,1:T(8,128)}), f32[2048,128]{0,1:T(8,128)}) %all-reduce.69.cloned.1.call-update) | async-done | bytes 1048592 | tf_op jit(solution)/shard_map/psum | solution.py:21
  1544.4 17.4 convolution_bitcast_fusion.7
  1561.9 102.4 %all-reduce.71.cloned.1.call-done = f32[8192,128]{0,1:T(8,128)} async-done(((f32[8192,128]{0,1:T(8,128)}), f32[8192,128]{0,1:T(8,128)}) %all-reduce.71.cloned.1.call-update) | async-done | bytes 4194320 | tf_op jit(solution)/shard_map/psum | solution.py:18
  1664.4 17.4 convolution_bitcast_fusion.23
  1681.8 30.9 %all-reduce.73.cloned.1.call-done = f32[2048,128]{0,1:T(8,128)} async-done(((f32[2048,128]{0,1:T(8,128)}), f32[2048,128]{0,1:T(8,128)}) %all-reduce.73.cloned.1.call-update) | async-done | bytes 1048592 | tf_op jit(solution)/shard_map/psum | solution.py:21
  1732.0 102.2 %all-reduce.75.cloned.1.call-done = f32[8192,128]{0,1:T(8,128)} async-done(((f32[8192,128]{0,1:T(8,128)}), f32[8192,128]{0,1:T(8,128)}) %all-reduce.75.cloned.1.call-update) | async-done | bytes 4194320 | tf_op jit(solution)/shard_map/psum | solution.py:18
  1834.2 17.4 convolution_bitcast_fusion.22
  1851.7 30.9 %all-reduce.77.cloned.1.call-done = f32[2048,128]{0,1:T(8,128)} async-done(((f32[2048,128]{0,1:T(8,128)}), f32[2048,128]{0,1:T(8,128)}) %all-reduce.77.cloned.1.call-update) | async-done | bytes 1048592 | tf_op jit(solution)/shard_map/psum | solution.py:21
  1885.7 17.4 convolution_bitcast_fusion.5
  1903.2 102.4 %all-reduce.79.cloned.1.call-done = f32[8192,128]{0,1:T(8,128)} async-done(((f32[8192,128]{0,1:T(8,128)}), f32[8192,128]{0,1:T(8,128)}) %all-reduce.79.cloned.1.call-update) | async-done | bytes 4194320 | tf_op jit(solution)/shard_map/psum | solution.py:18
  2005.6 17.4 convolution_bitcast_fusion.21
  2023.5 30.5 %all-reduce.81.cloned.1.call-done = f32[2048,128]{0,1:T(8,128)} async-done(((f32[2048,128]{0,1:T(8,128)}), f32[2048,128]{0,1:T(8,128)}) %all-reduce.81.cloned.1.call-update) | async-done | bytes 1048592 | tf_op jit(solution)/shard_map/psum | solution.py:21
  2073.1 102.4 %all-reduce.83.cloned.1.call-done = f32[8192,128]{0,1:T(8,128)} async-done(((f32[8192,128]{0,1:T(8,128)}), f32[8192,128]{0,1:T(8,128)}) %all-reduce.83.cloned.1.call-update) | async-done | bytes 4194320 | tf_op jit(solution)/shard_map/psum | solution.py:18
  2175.5 17.4 convolution_bitcast_fusion.20
  2193.0 30.9 %all-reduce.85.cloned.1.call-done = f32[2048,128]{0,1:T(8,128)} async-done(((f32[2048,128]{0,1:T(8,128)}), f32[2048,128]{0,1:T(8,128)}) %all-reduce.85.cloned.1.call-update) | async-done | bytes 1048592 | tf_op jit(solution)/shard_map/psum | solution.py:21
  2227.0 17.4 convolution_bitcast_fusion.3
  2244.6 102.3 %all-reduce.87.cloned.1.call-done = f32[8192,128]{0,1:T(8,128)} async-done(((f32[8192,128]{0,1:T(8,128)}), f32[8192,128]{0,1:T(8,128)}) %all-reduce.87.cloned.1.call-update) | async-done | bytes 4194320 | tf_op jit(solution)/shard_map/psum | solution.py:18
  2346.9 17.4 convolution_bitcast_fusion.19
  2364.4 30.9 %all-reduce.89.cloned.1.call-done = f32[2048,128]{0,1:T(8,128)} async-done(((f32[2048,128]{0,1:T(8,128)}), f32[2048,128]{0,1:T(8,128)}) %all-reduce.89.cloned.1.call-update) | async-done | bytes 1048592 | tf_op jit(solution)/shard_map/psum | solution.py:21
  2414.4 102.4 %all-reduce.91.cloned.1.call-done = f32[8192,128]{0,1:T(8,128)} async-done(((f32[8192,128]{0,1:T(8,128)}), f32[8192,128]{0,1:T(8,128)}) %all-reduce.91.cloned.1.call-update) | async-done | bytes 4194320 | tf_op jit(solution)/shard_map/psum | solution.py:18
  2516.8 17.4 convolution_bitcast_fusion.18
  2534.5 30.7 %all-reduce.93.cloned.1.call-done = f32[2048,128]{0,1:T(8,128)} async-done(((f32[2048,128]{0,1:T(8,128)}), f32[2048,128]{0,1:T(8,128)}) %all-reduce.93.cloned.1.call-update) | async-done | bytes 1048592 | tf_op jit(solution)/shard_map/psum | solution.py:21
  2568.2 17.4 convolution_bitcast_fusion.1
  2585.7 102.4 %all-reduce.95.cloned.1.call-done = f32[8192,128]{0,1:T(8,128)} async-done(((f32[8192,128]{0,1:T(8,128)}), f32[8192,128]{0,1:T(8,128)}) %all-reduce.95.cloned.1.call-update) | async-done | bytes 4194320 | tf_op jit(solution)/shard_map/psum | solution.py:18
  2688.2 17.4 convolution_bitcast_fusion.17
  2705.6 30.9 %all-reduce.97.cloned.1.call-done = f32[2048,128]{0,1:T(8,128)} async-done(((f32[2048,128]{0,1:T(8,128)}), f32[2048,128]{0,1:T(8,128)}) %all-reduce.97.cloned.1.call-update) | async-done | bytes 1048592 | tf_op jit(solution)/shard_map/psum | solution.py:21
  2738.3 17.4 convolution_bitcast_fusion
  2756.0 102.2 %all-reduce.99.cloned.1.call-done = f32[8192,128]{0,1:T(8,128)} async-done(((f32[8192,128]{0,1:T(8,128)}), f32[8192,128]{0,1:T(8,128)}) %all-reduce.99.cloned.1.call-update) | async-done | bytes 4194320 | tf_op jit(solution)/shard_map/psum | solution.py:18
  2858.2 17.4 convolution_bitcast_fusion.16
  2888.4 18.2 all-reduce.101.cloned.1.call-done
  (133 shorter events, 134.5 us)
Async XLA Ops:
  7.2 123.1 %all-reduce.35.cloned.1.call-start = ((), (), s32[]{:S(2)}) async-start(), calls=%async_computation | async-start | bytes 8388608 | tf_op jit(solution)/shard_map/psum | solution.py:18
  25.2 0.8 copy-start.14
  25.2 153.5 %all-reduce.37.cloned.1.call-start = ((), (), s32[]{:S(2)}) async-start(), calls=%async_computation.1 | async-start | bytes 2097152 | tf_op jit(solution)/shard_map/psum | solution.py:21
  25.9 121.8 %copy-start.12 = (f32[2048,128]{1,0:T(8,128)S(1)}, f32[2048,128]{1,0:T(8,128)}, u32[]{:S(2)}) copy-start(f32[2048,128]{1,0:T(8,128)} %param.7) | copy-start | bytes 3145732
  147.6 2.0 copy-start.13
  147.7 151.7 %all-reduce.39.cloned.1.call-start = ((), (), s32[]{:S(2)}) async-start(), calls=%async_computation.2 | async-start | bytes 8388608 | tf_op jit(solution)/shard_map/psum | solution.py:18
  149.6 198.1 %copy-start.11 = (f32[2048,128]{0,1:T(8,128)}, f32[2048,128]{0,1:T(8,128)S(1)}, u32[]{:S(2)}) copy-start(f32[2048,128]{0,1:T(8,128)S(1)} %copy.9) | copy-start | bytes 3145732
  149.7 368.5 %copy-start.15 = (f32[128]{0:T(128)}, f32[128]{0:T(128)S(1)}, u32[]{:S(2)}) copy-start(f32[128]{0:T(128)S(1)} %broadcast_multiply_fusion) | copy-start | bytes 1540
  196.9 150.9 %all-reduce.41.cloned.1.call-start = ((), (), s32[]{:S(2)}) async-start(), calls=%async_computation.3 | async-start | bytes 2097152 | tf_op jit(solution)/shard_map/psum | solution.py:21
  316.7 153.0 %all-reduce.43.cloned.1.call-start = ((), (), s32[]{:S(2)}) async-start(), calls=%async_computation.4 | async-start | bytes 8388608 | tf_op jit(solution)/shard_map/psum | solution.py:18
  367.2 150.9 %all-reduce.45.cloned.1.call-start = ((), (), s32[]{:S(2)}) async-start(), calls=%async_computation.5 | async-start | bytes 2097152 | tf_op jit(solution)/shard_map/psum | solution.py:21
  487.1 154.2 %all-reduce.47.cloned.1.call-start = ((), (), s32[]{:S(2)}) async-start(), calls=%async_computation.6 | async-start | bytes 8388608 | tf_op jit(solution)/shard_map/psum | solution.py:18
  521.0 168.7 %copy-start.10 = (f32[2048,128]{0,1:T(8,128)}, f32[2048,128]{0,1:T(8,128)S(1)}, u32[]{:S(2)}) copy-start(f32[2048,128]{0,1:T(8,128)S(1)} %multiply_add_fusion.28) | copy-start | bytes 3145732
  538.8 150.9 %all-reduce.49.cloned.1.call-start = ((), (), s32[]{:S(2)}) async-start(), calls=%async_computation.7 | async-start | bytes 2097152 | tf_op jit(solution)/shard_map/psum | solution.py:21
  658.7 152.5 %all-reduce.51.cloned.1.call-start = ((), (), s32[]{:S(2)}) async-start(), calls=%async_computation.8 | async-start | bytes 8388608 | tf_op jit(solution)/shard_map/psum | solution.py:18
  708.7 150.9 %all-reduce.53.cloned.1.call-start = ((), (), s32[]{:S(2)}) async-start(), calls=%async_computation.9 | async-start | bytes 2097152 | tf_op jit(solution)/shard_map/psum | solution.py:21
  828.6 153.2 %all-reduce.55.cloned.1.call-start = ((), (), s32[]{:S(2)}) async-start(), calls=%async_computation.10 | async-start | bytes 8388608 | tf_op jit(solution)/shard_map/psum | solution.py:18
  879.4 150.9 %all-reduce.57.cloned.1.call-start = ((), (), s32[]{:S(2)}) async-start(), calls=%async_computation.11 | async-start | bytes 2097152 | tf_op jit(solution)/shard_map/psum | solution.py:21
  999.2 152.5 %all-reduce.59.cloned.1.call-start = ((), (), s32[]{:S(2)}) async-start(), calls=%async_computation.12 | async-start | bytes 8388608 | tf_op jit(solution)/shard_map/psum | solution.py:18
  1049.2 150.9 %all-reduce.61.cloned.1.call-start = ((), (), s32[]{:S(2)}) async-start(), calls=%async_computation.13 | async-start | bytes 2097152 | tf_op jit(solution)/shard_map/psum | solution.py:21
  1169.1 154.0 %all-reduce.63.cloned.1.call-start = ((), (), s32[]{:S(2)}) async-start(), calls=%async_computation.14 | async-start | bytes 8388608 | tf_op jit(solution)/shard_map/psum | solution.py:18
  1202.2 1.0 copy-start
  1220.6 150.9 %copy-start.1 = (f32[2048,128]{0,1:T(8,128)S(1)}, f32[2048,128]{0,1:T(8,128)}, u32[]{:S(2)}) copy-start(f32[2048,128]{0,1:T(8,128)} %copy-done) | copy-start | bytes 3145732
  1220.6 150.9 %all-reduce.65.cloned.1.call-start = ((), (), s32[]{:S(2)}) async-start(), calls=%async_computation.15 | async-start | bytes 2097152 | tf_op jit(solution)/shard_map/psum | solution.py:21
  1340.5 152.5 %all-reduce.67.cloned.1.call-start = ((), (), s32[]{:S(2)}) async-start(), calls=%async_computation.16 | async-start | bytes 8388608 | tf_op jit(solution)/shard_map/psum | solution.py:18
  1390.5 150.9 %all-reduce.69.cloned.1.call-start = ((), (), s32[]{:S(2)}) async-start(), calls=%async_computation.17 | async-start | bytes 2097152 | tf_op jit(solution)/shard_map/psum | solution.py:21
  1510.4 154.0 %all-reduce.71.cloned.1.call-start = ((), (), s32[]{:S(2)}) async-start(), calls=%async_computation.18 | async-start | bytes 8388608 | tf_op jit(solution)/shard_map/psum | solution.py:18
  1543.5 1.0 copy-start.2
  1561.9 150.9 %copy-start.3 = (f32[2048,128]{0,1:T(8,128)S(1)}, f32[2048,128]{0,1:T(8,128)}, u32[]{:S(2)}) copy-start(f32[2048,128]{0,1:T(8,128)} %copy-done.2) | copy-start | bytes 3145732
  1561.9 150.9 %all-reduce.73.cloned.1.call-start = ((), (), s32[]{:S(2)}) async-start(), calls=%async_computation.19 | async-start | bytes 2097152 | tf_op jit(solution)/shard_map/psum | solution.py:21
  1681.8 152.5 %all-reduce.75.cloned.1.call-start = ((), (), s32[]{:S(2)}) async-start(), calls=%async_computation.20 | async-start | bytes 8388608 | tf_op jit(solution)/shard_map/psum | solution.py:18
  1731.8 150.9 %all-reduce.77.cloned.1.call-start = ((), (), s32[]{:S(2)}) async-start(), calls=%async_computation.21 | async-start | bytes 2097152 | tf_op jit(solution)/shard_map/psum | solution.py:21
  1851.7 154.0 %all-reduce.79.cloned.1.call-start = ((), (), s32[]{:S(2)}) async-start(), calls=%async_computation.22 | async-start | bytes 8388608 | tf_op jit(solution)/shard_map/psum | solution.py:18
  1884.7 1.0 copy-start.4
  1903.1 150.9 %copy-start.5 = (f32[2048,128]{0,1:T(8,128)S(1)}, f32[2048,128]{0,1:T(8,128)}, u32[]{:S(2)}) copy-start(f32[2048,128]{0,1:T(8,128)} %copy-done.4) | copy-start | bytes 3145732
  1903.1 150.9 %all-reduce.81.cloned.1.call-start = ((), (), s32[]{:S(2)}) async-start(), calls=%async_computation.23 | async-start | bytes 2097152 | tf_op jit(solution)/shard_map/psum | solution.py:21
  2023.1 152.5 %all-reduce.83.cloned.1.call-start = ((), (), s32[]{:S(2)}) async-start(), calls=%async_computation.24 | async-start | bytes 8388608 | tf_op jit(solution)/shard_map/psum | solution.py:18
  2073.0 150.9 %all-reduce.85.cloned.1.call-start = ((), (), s32[]{:S(2)}) async-start(), calls=%async_computation.25 | async-start | bytes 2097152 | tf_op jit(solution)/shard_map/psum | solution.py:21
  2192.9 154.0 %all-reduce.87.cloned.1.call-start = ((), (), s32[]{:S(2)}) async-start(), calls=%async_computation.26 | async-start | bytes 8388608 | tf_op jit(solution)/shard_map/psum | solution.py:18
  2226.0 1.0 copy-start.6
  2244.4 150.9 %copy-start.7 = (f32[2048,128]{0,1:T(8,128)S(1)}, f32[2048,128]{0,1:T(8,128)}, u32[]{:S(2)}) copy-start(f32[2048,128]{0,1:T(8,128)} %copy-done.6) | copy-start | bytes 3145732
  2244.4 150.9 %all-reduce.89.cloned.1.call-start = ((), (), s32[]{:S(2)}) async-start(), calls=%async_computation.27 | async-start | bytes 2097152 | tf_op jit(solution)/shard_map/psum | solution.py:21
  2364.3 152.5 %all-reduce.91.cloned.1.call-start = ((), (), s32[]{:S(2)}) async-start(), calls=%async_computation.28 | async-start | bytes 8388608 | tf_op jit(solution)/shard_map/psum | solution.py:18
  2414.3 150.9 %all-reduce.93.cloned.1.call-start = ((), (), s32[]{:S(2)}) async-start(), calls=%async_computation.29 | async-start | bytes 2097152 | tf_op jit(solution)/shard_map/psum | solution.py:21
  2534.2 154.0 %all-reduce.95.cloned.1.call-start = ((), (), s32[]{:S(2)}) async-start(), calls=%async_computation.30 | async-start | bytes 8388608 | tf_op jit(solution)/shard_map/psum | solution.py:18
  2567.3 1.0 copy-start.8
  2585.7 150.9 %copy-start.9 = (f32[2048,128]{0,1:T(8,128)S(1)}, f32[2048,128]{0,1:T(8,128)}, u32[]{:S(2)}) copy-start(f32[2048,128]{0,1:T(8,128)} %copy-done.8) | copy-start | bytes 3145732
  2585.7 150.9 %all-reduce.97.cloned.1.call-start = ((), (), s32[]{:S(2)}) async-start(), calls=%async_computation.31 | async-start | bytes 2097152 | tf_op jit(solution)/shard_map/psum | solution.py:21
  2705.6 152.6 %all-reduce.99.cloned.1.call-start = ((), (), s32[]{:S(2)}) async-start(), calls=%async_computation.32 | async-start | bytes 8388608 | tf_op jit(solution)/shard_map/psum | solution.py:18
  2755.7 150.9 %all-reduce.101.cloned.1.call-start = ((), (), s32[]{:S(2)}) async-start(), calls=%async_computation.33 | async-start | bytes 2097152 | tf_op jit(solution)/shard_map/psum | solution.py:21
  2875.6 31.0 %copy-start.16 = (f32[128]{0:T(128)S(1)}, f32[128]{0:T(128)}, u32[]{:S(2)}) copy-start(f32[128]{0:T(128)} %copy-done.15) | copy-start | bytes 1540
Sparse Core Ops, SparseCore 0:
  25.3 104.8 all-reduce.34
  147.8 30.8 all-reduce.36
  197.0 102.3 all-reduce.38
  316.9 30.8 all-reduce.40
  367.3 102.3 all-reduce.42
  487.2 30.8 all-reduce.44
  538.9 102.3 all-reduce.46
  658.8 30.8 all-reduce.48
  708.8 102.3 all-reduce.50
  828.7 30.7 all-reduce.52
  879.5 102.3 all-reduce.54
  999.4 30.8 all-reduce.56
  1049.3 102.3 all-reduce.58
  1169.2 30.8 all-reduce.60
  1220.7 102.3 all-reduce.62
  1340.6 30.8 all-reduce.64
  1390.6 102.3 all-reduce.66
  1510.5 30.8 all-reduce.68
  1562.0 102.3 all-reduce.70
  1681.9 30.8 all-reduce.72
  1731.9 102.3 all-reduce.74
  1851.8 30.8 all-reduce.76
  1903.3 102.3 all-reduce.78
  2023.2 30.8 all-reduce.80
  2073.2 102.3 all-reduce.82
  2193.1 30.8 all-reduce.84
  2244.5 102.3 all-reduce.86
  2364.4 30.8 all-reduce.88
  2414.4 102.3 all-reduce.90
  2534.3 30.8 all-reduce.92
  2585.8 102.3 all-reduce.94
  2705.7 30.8 all-reduce.96
  2755.8 102.3 all-reduce.98
  2875.7 30.8 all-reduce.100
where the time goes:
time: 2930 us; the launch traced here: 2920 us
  waiting for transfers between devices  2250 us (77%)
  matrix products  593 us (20%)
  other arithmetic  37.3 us (1%)
    psum x17, waiting for transfers between devices, gradient_at(): logits = lax.psum(part_logits, 'feat')  1740 us
    psum x17, waiting for transfers between devices, gradient_at(): return (lax.psum(local_grad, 'data') - position / PRIOR_VAR, logits)  510 us
    dot_general x17, matrix products, gradient_at(): jnp.dot(x_local, position.astype(jnp.bfloat16), preferred_element_type=jn...  297 us
    dot_general x17, matrix products, gradient_at(): lax.dot_general(x_local, residual, (((0,), (0,)), ((), ())), preferred_el...  296 us
  transfers between devices with their start and end apart: 34, of which 34 were waited for; matrix products, arithmetic and copies ran while one was open for 0% of the time, Pallas kernels for 0%

commit v1 on v0

v1 whole, which is shorter than its diff:
```python
import functools

import jax
import jax.numpy as jnp
from jax import lax
from jax.experimental import pallas as pl
from jax.experimental.pallas import tpu as pltpu
from jax.sharding import PartitionSpec as P

LEAPS = 16
PRIOR_VAR = 4.0
MESH = pl.DeviceIdType.MESH
LANES = 128
F32 = jnp.float32
BF16 = jnp.bfloat16


def contract_last(a, b):
    return lax.dot_general(a, b, (((1,), (1,)), ((), ())), preferred_element_type=F32)


def hmc_kernel(x_hbm, lab_ref, theta_ref, mom_ref, eps_ref,
               th_out, mo_out, en_out,
               xv, zt, rt, gb, dd, hs, rs, tb, tf, pf, eb, ebuf,
               loc_sem, xs_s, xs_r, ds_s, ds_r, rs_s, rs_r, ag_s, ag_r, ad_s, ad_r,
               fx_s, fx_r, fd_s, fd_r, en_s, en_r):
    nb = tb.shape[0]
    chains = zt.shape[1]
    n_zc, z_rows = zt.shape[0], zt.shape[2]
    rows = n_zc * z_rows
    wide = 4 * LANES
    part = lax.axis_index("parts")
    y = lax.axis_index("feat")
    d = lax.axis_index("data")
    x = d // 2
    c = d % 2
    xo, yo, co = 1 - x, 1 - y, 1 - c
    x_nbr = (part, y, 2 * xo + c)
    y_nbr = (part, yo, 2 * x + c)
    diag = (part, yo, 2 * xo + c)
    core = (part, y, 2 * x + co)
    peers = (x_nbr, y_nbr, diag)
    me = 4 * y + d

    def remote(src, dst, s_sem, r_sem, dev):
        return pltpu.make_async_remote_copy(src_ref=src, dst_ref=dst, send_sem=s_sem, recv_sem=r_sem,
                                            device_id=dev, device_id_type=MESH)

    others = []
    for dy in range(2):
        for dd_ in range(4):
            if dy or dd_:
                others.append((part, (y + dy) % 2, (d + dd_) % 4))

    barrier = pltpu.get_barrier_semaphore()
    for dev in others:
        pl.semaphore_signal(barrier, inc=1, device_id=dev, device_id_type=MESH)
    pl.semaphore_wait(barrier, 7)

    def x_copy(i):
        n = rows // xs_s.shape[0]
        return remote(x_hbm.at[pl.ds(pl.multiple_of(yo * rows + i * n, n), n), :],
                      xv.at[y, pl.ds(pl.multiple_of(i * n, n), n), :], xs_s.at[i], xs_r.at[i], y_nbr)

    def d2d_copy(j):
        return remote(gb.at[j, co], dd.at[j], ds_s.at[j], ds_r.at[j], core)

    def rs_copy(j, k):
        src = (hs.at[j, y, xo], hs.at[j, yo, x], hs.at[j, yo, xo])[k]
        return remote(src, rs.at[j, k], rs_s.at[j, k], rs_r.at[j, k], peers[k])

    def ag_copy(j, k):
        return remote(tb.at[j, c, y, x], tb.at[j, c, y, x], ag_s.at[j, k], ag_r.at[j, k], peers[k])

    def agd_copy(j):
        return remote(tb.at[j, c], tb.at[j, c], ad_s.at[j], ad_r.at[j], core)

    eb[...] = jnp.broadcast_to(eps_ref[...], (LANES, chains)).T
    for j in range(nb):
        tile = theta_ref[j, c, x].T
        tf[j] = tile
        tb[j, c, y, x] = tile.astype(BF16)
        pf[j] = mom_ref[j, c, x].T
        for k in range(3):
            ag_copy(j, k).start()
    n_x = xs_s.shape[0]

    @pl.loop(0, n_x)
    def _(i):
        x_copy(i).start()

    local = pltpu.make_async_copy(x_hbm.at[pl.ds(pl.multiple_of(y * rows, rows), rows), :], xv.at[y], loc_sem)
    local.start()

    def gather_mid(j):
        for k in range(3):
            ag_copy(j, k).wait()
        agd_copy(j).start()

    def gather_end(j):
        agd_copy(j).wait()

    for j in range(nb):
        gather_mid(j)
    for j in range(nb):
        gather_end(j)
    local.wait()

    def lhs_of(j, h):
        return jnp.concatenate([tb[j, cc, h, xx] for cc in range(2) for xx in range(2)], axis=1)

    def residual(i, z):
        lab = lab_ref[:, pl.ds(pl.multiple_of(y * rows + i * z_rows, z_rows), z_rows)]
        rt[:, pl.ds(pl.multiple_of(i * z_rows, z_rows), z_rows)] = (lab - jax.nn.sigmoid(z)).astype(BF16)

    @pl.loop(0, n_x)
    def _(i):
        x_copy(i).wait_recv()
        n = rows // n_x
        at = pl.ds(pl.multiple_of(i * n, n), n)
        acc = jnp.zeros((chains, n), F32)
        for j in range(nb):
            for h in range(2):
                acc = acc + contract_last(lhs_of(j, h), xv[h, at, j * wide:(j + 1) * wide])
        lab = lab_ref[:, pl.ds(pl.multiple_of(y * rows + i * n, n), n)]
        rt[:, at] = (lab - jax.nn.sigmoid(acc)).astype(BF16)

    @pl.loop(0, n_x)
    def _(i):
        x_copy(i).wait_send()

    def grad_block(j):
        cols = pl.ds(pl.multiple_of(j * wide, wide), wide)
        for h in range(2):
            out = jnp.dot(rt[...], xv[h, :, cols], preferred_element_type=F32)
            for cc in range(2):
                for xx in range(2):
                    k = 2 * cc + xx
                    gb[j, cc, h, xx] = out[:, k * LANES:(k + 1) * LANES]
        d2d_copy(j).start()

    def pair_sum(j):
        d2d_copy(j).wait()
        hs[j] = gb[j, c] + dd[j]
        for k in range(3):
            rs_copy(j, k).start()

    def update(j, t):
        for k in range(3):
            rs_copy(j, k).wait()
        total = (hs[j, y, x] + rs[j, 0]) + (rs[j, 1] + rs[j, 2])
        pos = tf[j]
        ends = jnp.logical_or(t == 0, t == LEAPS)
        scale = eb[...] * jnp.where(ends, 0.5, 1.0)
        mom = pf[j] + scale * (total - pos / PRIOR_VAR)
        pf[j] = mom

        @pl.when(t < LEAPS)
        def _():
            new = pos + eb[...] * mom
            tf[j] = new
            tb[j, c, y, x] = new.astype(BF16)
            for k in range(3):
                ag_copy(j, k).start()

    def logits_block(j):
        cols = pl.ds(pl.multiple_of(j * wide, wide), wide)
        left = [lhs_of(j, h) for h in range(2)]

        @pl.loop(0, n_zc)
        def _(i):
            at = pl.ds(pl.multiple_of(i * z_rows, z_rows), z_rows)
            new = contract_last(left[0], xv[0, at, cols]) + contract_last(left[1], xv[1, at, cols])
            zt[i] = jnp.where(j == 0, 0.0, zt[i]) + new

    d_mid, d_upd, d_gat, d_log = 1, 3, 4, 5

    def one_eval(t, carry):
        steps = jnp.where(t < LEAPS, nb + d_log, nb + d_upd)

        def step(s, carry):
            def on(delay, fn, *args):
                @pl.when(jnp.logical_and(s >= delay, s < nb + delay))
                def _():
                    fn(s - delay, *args)

            on(0, grad_block)
            on(d_mid, pair_sum)
            on(d_upd, update, t)

            @pl.when(t < LEAPS)
            def _():
                on(d_gat, gather_mid)

                @pl.when(jnp.logical_and(s >= d_log, s < nb + d_log))
                def _():
                    gather_end(s - d_log)
                    logits_block(s - d_log)

                @pl.when(s == nb + d_log - 1)
                def _():
                    @pl.loop(0, n_zc)
                    def _(i):
                        residual(i, zt[i])
            return carry

        return lax.fori_loop(0, steps, step, carry)

    lax.fori_loop(0, LEAPS + 1, one_eval, 0)

    for j in range(nb):
        th_out[j, c, x] = tf[j].T
        mo_out[j, c, x] = pf[j].T
    outs = (th_out, mo_out)
    fx = [remote(o.at[:, c, x], o.at[:, c, x], fx_s.at[n], fx_r.at[n], x_nbr) for n, o in enumerate(outs)]
    for cp in fx:
        cp.start()

    def loss(i, acc):
        z = zt[i]
        lab = lab_ref[:, pl.ds(pl.multiple_of(y * rows + i * z_rows, z_rows), z_rows)]
        soft = jnp.maximum(z, 0.0) + jnp.log1p(jnp.exp(-jnp.abs(z)))
        term = soft - lab * z
        for q in range(z_rows // LANES):
            acc = acc + term[:, q * LANES:(q + 1) * LANES]
        return acc

    acc = lax.fori_loop(0, n_zc, loss, jnp.zeros((chains, LANES), F32))
    for j in range(nb):
        acc = acc + tf[j] * tf[j] * (1.0 / (2.0 * PRIOR_VAR)) + 0.5 * (pf[j] * pf[j])
    row = jnp.sum(acc.T, axis=0, keepdims=True)
    ebuf[me] = jnp.broadcast_to(row, (8, chains))
    sends = []
    for n, dev in enumerate(others):
        cp = remote(ebuf.at[me], ebuf.at[me], en_s.at[n], en_r.at[n], dev)
        cp.start()
        sends.append(cp)

    for cp in fx:
        cp.wait()
    fd = [remote(o.at[:, c], o.at[:, c], fd_s.at[n], fd_r.at[n], core) for n, o in enumerate(outs)]
    for cp in fd:
        cp.start()
    for cp in sends:
        cp.wait()
    total = ebuf[0]
    for n in range(1, 8):
        total = total + ebuf[n]
    en_out[...] = total[0:1]
    for cp in fd:
        cp.wait()


def solution(mesh):
    chain_spec = P("feat", "parts")

    def local_run(x_local, labels, theta_init, mom_init, step_size):
        n_local, feats_half = x_local.shape
        rows = n_local // 2
        chains = theta_init.shape[1]
        nb = feats_half // (4 * LANES)
        z_rows = min(4096, rows)
        n_x = 16
        tiles = (nb, 2, 2, LANES, chains)
        vm = pl.BlockSpec(memory_space=pltpu.VMEM)
        dma = pltpu.SemaphoreType.DMA
        th, mo, en = pl.pallas_call(
            hmc_kernel,
            out_shape=(jax.ShapeDtypeStruct(tiles, F32), jax.ShapeDtypeStruct(tiles, F32),
                       jax.ShapeDtypeStruct((1, chains), F32)),
            in_specs=[pl.BlockSpec(memory_space=pl.ANY), vm, vm, vm, vm],
            out_specs=(vm, vm, vm),
            scratch_shapes=[
                pltpu.VMEM((2, rows, feats_half), BF16),
                pltpu.VMEM((rows // z_rows, chains, z_rows), F32),
                pltpu.VMEM((chains, rows), BF16),
                pltpu.VMEM((nb, 2, 2, 2, chains, LANES), F32),
                pltpu.VMEM((nb, 2, 2, chains, LANES), F32),
                pltpu.VMEM((nb, 2, 2, chains, LANES), F32),
                pltpu.VMEM((nb, 3, chains, LANES), F32),
                pltpu.VMEM((nb, 2, 2, 2, chains, LANES), BF16),
                pltpu.VMEM((nb, chains, LANES), F32),
                pltpu.VMEM((nb, chains, LANES), F32),
                pltpu.VMEM((chains, LANES), F32),
                pltpu.VMEM((8, 8, chains), F32),
                dma, dma((n_x,)), dma((n_x,)), dma((nb,)), dma((nb,)), dma((nb, 3)), dma((nb, 3)),
                dma((nb, 3)), dma((nb, 3)), dma((nb,)), dma((nb,)),
                dma((2,)), dma((2,)), dma((2,)), dma((2,)), dma((7,)), dma((7,)),
            ],
            compiler_params=pltpu.CompilerParams(collective_id=0, has_side_effects=True,
                                                 vmem_limit_bytes=62 * 1024 * 1024),
        )(x_local, labels.astype(F32)[None, :], theta_init.reshape(tiles), mom_init.reshape(tiles),
          step_size[None, :])
        return th.reshape(theta_init.shape), mo.reshape(theta_init.shape), en.reshape(chains)

    return jax.shard_map(local_run, mesh=mesh,
                         in_specs=(P("data", "feat"), P("data"), chain_spec, chain_spec, P("parts")),
                         out_specs=(chain_spec, chain_spec, P("parts")), check_vma=False)
```

time: 2930 us -> 935 us (0.32)
  waiting for transfers between devices: 2250 us -> 0 us
  Pallas kernels: 0 us -> 927 us
  matrix products: 593 us -> 0 us
  other arithmetic: 37.3 us -> 1.38 us
    psum x34 -> x0, waiting for transfers between devices: 2250 us -> none  [the longest x17 1740 us: gradient_at(): logits = lax.psum(part_logits, 'feat')]
    pallas_call x0 -> x1, Pallas kernels: none -> 927 us  [local_run(): pl.pallas_call(hmc_kernel, out_shape=(jax.ShapeDtypeStruct(tiles, F32), j...]
    dot_general x34 -> x0, matrix products: 593 us -> none  [the longest x17 297 us: gradient_at(): jnp.dot(x_local, position.astype(jnp.bfloat16), preferred_element_type=jn...]
  transfers between devices with their start and end apart: 34 -> 0, of which waited for: 34 -> 0; matrix products, arithmetic and copies ran while one was open for 0% -> 0% of each run, Pallas kernels for 0% -> 0%
where the time goes in v1:
time: 935 us
  Pallas kernels  927 us (99%)
    pallas_call x1, Pallas kernels, local_run(): pl.pallas_call(hmc_kernel, out_shape=(jax.ShapeDtypeStruct(tiles, F32), j...  927 us

profile of v1, /device:TPU:0, one launch (start us, length us, event | category | flops | bytes accessed | tf_op | source)
XLA Modules:
  0.0 935.1 jit_solution(448362186828580894)
XLA Ops:
  0.6 1.4 convert_element_type.3
  2.0 927.4 %shard_map.76 = (f32[4,2,2,128,128]{4,3,2,1,0:T(8,128)}, f32[4,2,2,128,128]{4,3,2,1,0:T(8,128)}, f32[1,128]{1,0:T(1,128)}) custom-call(bf16[8192,2048]{1,0:T(8,128)(2,1)} %x_hbm.1, f32[1,8192]{1,0:T(1,128)} %bitcast.11, f32[4,2,2,128,128]{4,3,2,1,0:T(8,128)} %bitcast.7, f32[4,2,2,128,128]{4,3,2,1,0:T(8,128)} %bitcast.8, f32[1,128]{1,0:T(1,128)} %bitcast.12), custom_call_target="tpu_custom_call" | custom-call | tf_op jit(solution)/shard_map/pallas_call | solution.py:267
  929.4 2.3 copy.11
  931.7 2.3 copy.12
  934.0 1.1 copy.13

commit v2 on v1

v2 whole, which is shorter than its diff:
```python
import functools

import jax
import jax.numpy as jnp
from jax import lax
from jax.experimental import pallas as pl
from jax.experimental.pallas import tpu as pltpu
from jax.sharding import PartitionSpec as P

LEAPS = 16
PRIOR_VAR = 4.0
MESH = pl.DeviceIdType.MESH
LANES = 128
F32 = jnp.float32
BF16 = jnp.bfloat16


def contract_last(a, b):
    return lax.dot_general(a, b, (((1,), (1,)), ((), ())), preferred_element_type=F32)


def hmc_kernel(x_hbm, lab_ref, theta_ref, mom_ref, eps_ref,
               th_out, mo_out, en_out,
               xv, xw, zt, rt, gb, dd, r1, h2, r2, tb, tf, pf, xt, eb, lsum, ebuf,
               loc_sem, io_sem, xs_s, xs_r, in_s, in_r, ds_s, ds_r, r1_s, r1_r, r2_s, r2_r, a1_s, a1_r, ad_s, ad_r,
               fx_s, fx_r, fd_s, fd_r, en_s, en_r):
    nb = tb.shape[0]
    chains = zt.shape[1]
    n_zc, z_rows = zt.shape[0], zt.shape[2]
    rows = n_zc * z_rows
    wide = 4 * LANES
    part = lax.axis_index("parts")
    y = lax.axis_index("feat")
    d = lax.axis_index("data")
    x = d // 2
    c = d % 2
    xo, yo, co = 1 - x, 1 - y, 1 - c
    x_nbr = (part, y, 2 * xo + c)
    y_nbr = (part, yo, 2 * x + c)
    core = (part, y, 2 * x + co)
    pair = (x_nbr, y_nbr)
    half = chains // 2
    me = 4 * y + d

    def remote(src, dst, s_sem, r_sem, dev):
        return pltpu.make_async_remote_copy(src_ref=src, dst_ref=dst, send_sem=s_sem, recv_sem=r_sem,
                                            device_id=dev, device_id_type=MESH)

    others = []
    for dy in range(2):
        for dd_ in range(4):
            if dy or dd_:
                others.append((part, (y + dy) % 2, (d + dd_) % 4))

    barrier = pltpu.get_barrier_semaphore()
    for dev in others:
        pl.semaphore_signal(barrier, inc=1, device_id=dev, device_id_type=MESH)
    pl.semaphore_wait(barrier, 7)

    def x_copy(i):
        n = rows // xs_s.shape[0]
        return remote(x_hbm.at[pl.ds(pl.multiple_of(yo * rows + i * n, n), n), :],
                      xv.at[y, pl.ds(pl.multiple_of(i * n, n), n), :], xs_s.at[i], xs_r.at[i], y_nbr)

    def d2d_copy(j):
        return remote(gb.at[j, co], dd.at[j], ds_s.at[j], ds_r.at[j], core)

    def rs1_copy(j, k):
        src = (gb.at[j, c, :, xo, :half], gb.at[j, c, yo, :, half:])[k]
        return remote(src, r1.at[j, k], r1_s.at[j, k], r1_r.at[j, k], pair[k])

    def rs2_copy(j, k):
        return remote(h2.at[j, k], r2.at[j, k], r2_s.at[j, k], r2_r.at[j, k], pair[1 - k])

    def ag1_copy(j, k):
        ref = (tb.at[j, c, 0, :, x], tb.at[j, c, 1, y])[k]
        return remote(ref, ref, a1_s.at[j, k], a1_r.at[j, k], pair[k])

    def start_copy(n):
        ref = (tf, pf)[n].at[:, 0, y]
        return remote(ref, ref, in_s.at[n], in_r.at[n], y_nbr)

    def last_copy(n):
        return remote((tf, pf)[n].at[:, 0, y], xt.at[n], fx_s.at[n], fx_r.at[n], x_nbr)

    def agd_copy(j):
        return remote(tb.at[j, c], tb.at[j, c], ad_s.at[j], ad_r.at[j], core)

    n_x = xs_s.shape[0]
    ahead = 2
    staged = [pltpu.make_async_copy(ref.at[:, c], gb.at[:, n, c], io_sem.at[n])
              for n, ref in enumerate((theta_ref, mom_ref))]
    for cp in staged:
        cp.start()
    for i in range(ahead):
        x_copy(i).start()
    local = pltpu.make_async_copy(x_hbm.at[pl.ds(pl.multiple_of(y * rows, rows), rows), :], xv.at[y], loc_sem)
    local.start()
    eb[...] = jnp.broadcast_to(eps_ref[...], (LANES, chains)).T
    for cp in staged:
        cp.wait()
    for j in range(nb):
        for xx in range(2):
            tf[j, 1, xx] = gb[j, 0, c, xx].T[half:]
            pf[j, 1, xx] = gb[j, 1, c, xx].T[half:]
            tb[j, c, 1, y, xx] = tf[j, 1, xx].astype(BF16)
        tf[j, 0, y] = gb[j, 0, c, x].T[:half]
        pf[j, 0, y] = gb[j, 1, c, x].T[:half]
    start_copy(0).start()
    for j in range(nb):
        ag1_copy(j, 1).start()

    @pl.loop(ahead, n_x)
    def _(i):
        x_copy(i).start()

    start_copy(1).start()

    def gather_mid(j):
        for k in range(2):
            ag1_copy(j, k).wait()
        agd_copy(j).start()

    def gather_end(j):
        agd_copy(j).wait()

    start_copy(0).wait()
    for j in range(nb):
        tb[j, c, 0, :, x] = tf[j, 0].astype(BF16)
        ag1_copy(j, 0).start()
    for j in range(nb):
        gather_mid(j)
    for j in range(nb):
        gather_end(j)
    local.wait()

    def lhs_of(j, h):
        top = jnp.concatenate([tb[j, cc, 0, h, xx] for cc in range(2) for xx in range(2)], axis=1)
        low = jnp.concatenate([tb[j, cc, 1, h, xx] for cc in range(2) for xx in range(2)], axis=1)
        return jnp.concatenate([top, low], axis=0)

    def label_row(i, n):
        return lab_ref[:, pl.ds(pl.multiple_of(y * rows + i * n, n), n)].astype(F32)

    def residual(i, z):
        lab = label_row(i, z_rows)
        rt[:, pl.ds(pl.multiple_of(i * z_rows, z_rows), z_rows)] = (lab - jax.nn.sigmoid(z)).astype(BF16)

    @pl.loop(0, n_x)
    def _(i):
        x_copy(i).wait_recv()
        n = rows // n_x
        at = pl.ds(pl.multiple_of(i * n, n), n)
        acc = jnp.zeros((chains, n), F32)
        for j in range(nb):
            for h in range(2):
                acc = acc + contract_last(lhs_of(j, h), xv[h, at, j * wide:(j + 1) * wide])
        lab = label_row(i, n)
        rt[:, at] = (lab - jax.nn.sigmoid(acc)).astype(BF16)
        for j in range(xw.shape[0]):
            for h in range(2):
                src = (nb - xw.shape[0] + j) * wide
                xw[j, h * wide:(h + 1) * wide, at] = xv[h, at, src:src + wide].T

    @pl.loop(0, n_x)
    def _(i):
        x_copy(i).wait_send()

    start_copy(1).wait()

    def grad_block(j):
        cols = pl.ds(pl.multiple_of(j * wide, wide), wide)
        for h in range(2):
            out = jnp.dot(rt[...], xv[h, :, cols], preferred_element_type=F32)
            for q in range(4):
                gb[j, q // 2, h, q % 2] = out[:, q * LANES:(q + 1) * LANES]
        d2d_copy(j).start()

    def pair_sum(j):
        d2d_copy(j).wait()
        gb[j, c] += dd[j]
        for k in range(2):
            rs1_copy(j, k).start()

    def chip_sum(j):
        for k in range(2):
            rs1_copy(j, k).wait()
        h2[j, 0] = gb[j, c, :, x, :half] + r1[j, 0]
        h2[j, 1] = gb[j, c, y, :, half:] + r1[j, 1]
        for k in range(2):
            rs2_copy(j, k).start()

    def update(j, t):
        for k in range(2):
            rs2_copy(j, k).wait()
        pos = tf[j]
        eps = eb[...].reshape(2, 1, half, LANES)
        ends = jnp.logical_or(t == 0, t == LEAPS)
        mom = pf[j] + eps * jnp.where(ends, 0.5, 1.0) * ((h2[j] + r2[j]) - pos / PRIOR_VAR)
        pf[j] = mom

        @pl.when(t < LEAPS)
        def _():
            new = pos + eps * mom
            tf[j] = new
            low = new.astype(BF16)
            tb[j, c, 0, :, x] = low[0]
            tb[j, c, 1, y] = low[1]
            for k in range(2):
                ag1_copy(j, k).start()

    n_slow = nb - xw.shape[0]

    def logits_block(j):
        left = [lhs_of(j, h) for h in range(2)]

        @pl.when(j < n_slow)
        def _():
            cols = pl.ds(pl.multiple_of(j * wide, wide), wide)

            @pl.loop(0, n_zc)
            def _(i):
                at = pl.ds(pl.multiple_of(i * z_rows, z_rows), z_rows)
                new = contract_last(left[0], xv[0, at, cols]) + contract_last(left[1], xv[1, at, cols])
                zt[i] = jnp.where(j == 0, 0.0, zt[i]) + new

        @pl.when(j >= n_slow)
        def _():
            both = jnp.concatenate(left, axis=1)

            @pl.loop(0, n_zc)
            def _(i):
                at = pl.ds(pl.multiple_of(i * z_rows, z_rows), z_rows)
                zt[i] += jnp.dot(both, xw[j - n_slow, :, at], preferred_element_type=F32)

    d_mid, d_chp, d_upd, d_gat, d_log = 1, 3, 4, 5, 6

    def loss(i, acc):
        z = zt[i]
        soft = jnp.maximum(z, 0.0) + jnp.log1p(jnp.exp(-jnp.abs(z)))
        term = soft - label_row(i, z_rows) * z
        for q in range(z_rows // LANES):
            acc = acc + term[:, q * LANES:(q + 1) * LANES]
        return acc

    def one_eval(t, carry):
        steps = jnp.where(t < LEAPS, nb + d_log, nb + d_upd)

        def step(s, carry):
            def on(delay, fn, *args):
                @pl.when(jnp.logical_and(s >= delay, s < nb + delay))
                def _():
                    fn(s - delay, *args)

            @pl.when(jnp.logical_and(t == LEAPS, s == 0))
            def _():
                last_copy(0).start()

            @pl.when(jnp.logical_and(t == LEAPS, s == nb))
            def _():
                lsum[...] = lax.fori_loop(0, n_zc, loss, jnp.zeros((chains, LANES), F32))

            on(0, grad_block)
            on(d_mid, pair_sum)
            on(d_chp, chip_sum)
            on(d_upd, update, t)

            @pl.when(t < LEAPS)
            def _():
                on(d_gat, gather_mid)

                @pl.when(jnp.logical_and(s >= d_log, s < nb + d_log))
                def _():
                    gather_end(s - d_log)
                    logits_block(s - d_log)

                @pl.when(s == nb + d_log - 1)
                def _():
                    @pl.loop(0, n_zc)
                    def _(i):
                        residual(i, zt[i])
            return carry

        return lax.fori_loop(0, steps, step, carry)

    lax.fori_loop(0, LEAPS + 1, one_eval, 0)

    last_copy(1).start()
    acc = lsum[...]
    for j in range(nb):
        for h in range(2):
            own = tf[j, 0, h] * tf[j, 0, h] * (1.0 / (2.0 * PRIOR_VAR)) + 0.5 * (pf[j, 0, h] * pf[j, 0, h])
            twin = tf[j, 1, h] * tf[j, 1, h] * (1.0 / (2.0 * PRIOR_VAR)) + 0.5 * (pf[j, 1, h] * pf[j, 1, h])
            acc = acc + jnp.concatenate([jnp.where(h == y, own, 0.0), jnp.where(h == x, twin, 0.0)], axis=0)
    row = jnp.sum(acc.T, axis=0, keepdims=True)
    ebuf[me] = jnp.broadcast_to(row, (8, chains))
    sends = []
    for n, dev in enumerate(others):
        cp = remote(ebuf.at[me], ebuf.at[me], en_s.at[n], en_r.at[n], dev)
        cp.start()
        sends.append(cp)

    for cp in sends:
        cp.wait()
    total = ebuf[0]
    for n in range(1, 8):
        total = total + ebuf[n]
    en_out[...] = total[0:1]

    def put(n, k):
        cc = (c, co)[k]
        return pltpu.make_async_copy(gb.at[:, n, cc], (th_out, mo_out)[n].at[:, cc], io_sem.at[2 * k + n])

    def swap(n):
        return remote(gb.at[:, n, c], gb.at[:, n, c], fd_s.at[n], fd_r.at[n], core)

    for n in range(2):
        last_copy(n).wait()
        state = (tf, pf)[n]
        for j in range(nb):
            gb[j, n, c, x] = jnp.concatenate([state[j, 0, y], state[j, 1, x]], axis=0).T
            gb[j, n, c, xo] = jnp.concatenate([xt[n, j], state[j, 1, xo]], axis=0).T
        swap(n).start()
        put(n, 0).start()
    for n in range(2):
        swap(n).wait()
        put(n, 1).start()
    for n in range(2):
        put(n, 0).wait()
        put(n, 1).wait()


def solution(mesh):
    chain_spec = P("feat", "parts")

    def local_run(x_local, labels, theta_init, mom_init, step_size):
        n_local, feats_half = x_local.shape
        rows = n_local // 2
        chains = theta_init.shape[1]
        nb = feats_half // (4 * LANES)
        z_rows = min(4096, rows)
        n_x = 16
        tiles = (nb, 2, 2, LANES, chains)
        vm = pl.BlockSpec(memory_space=pltpu.VMEM)
        dma = pltpu.SemaphoreType.DMA
        far = pl.BlockSpec(memory_space=pl.ANY)
        th, mo, en = pl.pallas_call(
            hmc_kernel,
            out_shape=(jax.ShapeDtypeStruct(tiles, F32), jax.ShapeDtypeStruct(tiles, F32),
                       jax.ShapeDtypeStruct((1, chains), F32)),
            in_specs=[far, vm, far, far, vm],
            out_specs=(far, far, vm),
            scratch_shapes=[
                pltpu.VMEM((2, rows, feats_half), BF16),
                pltpu.VMEM((nb // 2, 8 * LANES, rows), BF16),
                pltpu.VMEM((rows // z_rows, chains, z_rows), F32),
                pltpu.VMEM((chains, rows), BF16),
                pltpu.VMEM((nb, 2, 2, 2, chains, LANES), F32),
                pltpu.VMEM((nb, 2, 2, chains, LANES), F32),
                pltpu.VMEM((nb, 2, 2, chains // 2, LANES), F32),
                pltpu.VMEM((nb, 2, 2, chains // 2, LANES), F32),
                pltpu.VMEM((nb, 2, 2, chains // 2, LANES), F32),
                pltpu.VMEM((nb, 2, 2, 2, 2, chains // 2, LANES), BF16),
                pltpu.VMEM((nb, 2, 2, chains // 2, LANES), F32),
                pltpu.VMEM((nb, 2, 2, chains // 2, LANES), F32),
                pltpu.VMEM((2, nb, chains // 2, LANES), F32),
                pltpu.VMEM((chains, LANES), F32),
                pltpu.VMEM((chains, LANES), F32),
                pltpu.VMEM((8, 8, chains), F32),
                dma, dma((4,)), dma((n_x,)), dma((n_x,)), dma((2,)), dma((2,)), dma((nb,)), dma((nb,)),
                dma((nb, 2)), dma((nb, 2)), dma((nb, 2)), dma((nb, 2)),
                dma((nb, 2)), dma((nb, 2)), dma((nb,)), dma((nb,)),
                dma((2,)), dma((2,)), dma((2,)), dma((2,)), dma((7,)), dma((7,)),
            ],
            compiler_params=pltpu.CompilerParams(collective_id=0, has_side_effects=True,
                                                 vmem_limit_bytes=67043328),
        )(x_local, labels[None, :], theta_init.reshape(tiles), mom_init.reshape(tiles),
          step_size[None, :])
        return th.reshape(theta_init.shape), mo.reshape(theta_init.shape), en.reshape(chains)

    return jax.shard_map(local_run, mesh=mesh,
                         in_specs=(P("data", "feat"), P("data"), chain_spec, chain_spec, P("parts")),
                         out_specs=(chain_spec, chain_spec, P("parts")), check_vma=False)
```

time: 935 us -> 816 us (0.87)
  Pallas kernels: 927 us -> 809 us
    pallas_call x1, Pallas kernels: 927 us -> 809 us  [local_run(): pl.pallas_call(hmc_kernel, out_shape=(jax.ShapeDtypeStruct(tiles, F32), j...]
where the time goes in v2:
time: 816 us; the launch traced here: 815 us
  Pallas kernels  809 us (99%)
    pallas_call x1, Pallas kernels, local_run(): pl.pallas_call(hmc_kernel, out_shape=(jax.ShapeDtypeStruct(tiles, F32), j...  809 us

profile of v2, /device:TPU:0, one launch (start us, length us, event | category | flops | bytes accessed | tf_op | source)
XLA Modules:
  0.0 815.4 jit_solution(16648467594116715585)
XLA Ops:
  0.6 809.1 %shard_map.76 = (f32[4,2,2,128,128]{4,3,2,1,0:T(8,128)}, f32[4,2,2,128,128]{4,3,2,1,0:T(8,128)}, f32[1,128]{1,0:T(1,128)}) custom-call(bf16[8192,2048]{1,0:T(8,128)(2,1)} %x_hbm.1, s32[1,8192]{1,0:T(1,128)} %bitcast.11, f32[4,2,2,128,128]{4,3,2,1,0:T(8,128)} %bitcast.7, f32[4,2,2,128,128]{4,3,2,1,0:T(8,128)} %bitcast.8, f32[1,128]{1,0:T(1,128)} %bitcast.12), custom_call_target="tpu_custom_call" | custom-call | tf_op jit(solution)/shard_map/pallas_call | solution.py:347
  809.8 2.3 copy.11
  812.0 2.3 copy.12
  814.3 1.1 copy.13

commit v3 on v2

--- a/solution.py
+++ b/solution.py
@@ -11,6 +11,11 @@
 PRIOR_VAR = 4.0
 MESH = pl.DeviceIdType.MESH
 LANES = 128
+PLAN = (
+        "e0", "g0", "h0", "g1", "p0", "h1", "g2", "p1", "h2", "p2", "c0", "g3",
+        "c1", "h3", "p3", "l0", "u0", "c2", "c3", "u1", "m0", "o0", "u2", "t0",
+        "u3", "m1", "o1", "m2", "o2", "t1", "m3", "o3", "t2", "t3",
+)
 F32 = jnp.float32
 BF16 = jnp.bfloat16
 
@@ -21,7 +26,7 @@
 
 def hmc_kernel(x_hbm, lab_ref, theta_ref, mom_ref, eps_ref,
                th_out, mo_out, en_out,
-               xv, xw, zt, rt, gb, dd, r1, h2, r2, tb, tf, pf, xt, eb, lsum, ebuf,
+               xa, zt, rt, gb, dd, r1, h2, r2, tb, tf, pf, xt, eb, lsum, ebuf,
                loc_sem, io_sem, xs_s, xs_r, in_s, in_r, ds_s, ds_r, r1_s, r1_r, r2_s, r2_r, a1_s, a1_r, ad_s, ad_r,
                fx_s, fx_r, fd_s, fd_r, en_s, en_r):
     nb = tb.shape[0]
@@ -29,6 +34,8 @@
     n_zc, z_rows = zt.shape[0], zt.shape[2]
     rows = n_zc * z_rows
     wide = 4 * LANES
+    strip = 2 * LANES
+    n_x = 2 * nb
     part = lax.axis_index("parts")
     y = lax.axis_index("feat")
     d = lax.axis_index("data")
@@ -57,10 +64,15 @@
         pl.semaphore_signal(barrier, inc=1, device_id=dev, device_id_type=MESH)
     pl.semaphore_wait(barrier, 7)
 
-    def x_copy(i):
-        n = rows // xs_s.shape[0]
-        return remote(x_hbm.at[pl.ds(pl.multiple_of(yo * rows + i * n, n), n), :],
-                      xv.at[y, pl.ds(pl.multiple_of(i * n, n), n), :], xs_s.at[i], xs_r.at[i], y_nbr)
+    def strip_refs(u, here):
+        src = x_hbm.at[pl.ds(pl.multiple_of(here * rows, rows), rows), pl.ds(pl.multiple_of(u * strip, strip), strip)]
+        return src, xa.at[u, :, pl.ds(pl.multiple_of(y * strip, strip), strip)]
+
+    def x_copy(u):
+        return remote(*strip_refs(u, yo), xs_s.at[u], xs_r.at[u], y_nbr)
+
+    def x_local(u):
+        return pltpu.make_async_copy(*strip_refs(u, y), loc_sem.at[u])
 
     def d2d_copy(j):
         return remote(gb.at[j, co], dd.at[j], ds_s.at[j], ds_r.at[j], core)
@@ -80,22 +92,25 @@
         ref = (tf, pf)[n].at[:, 0, y]
         return remote(ref, ref, in_s.at[n], in_r.at[n], y_nbr)
 
-    def last_copy(n):
-        return remote((tf, pf)[n].at[:, 0, y], xt.at[n], fx_s.at[n], fx_r.at[n], x_nbr)
+    def last_copy(n, j):
+        return remote((tf, pf)[n].at[j, 0, y], xt.at[n, j], fx_s.at[n, j], fx_r.at[n, j], x_nbr)
 
     def agd_copy(j):
         return remote(tb.at[j, c], tb.at[j, c], ad_s.at[j], ad_r.at[j], core)
 
-    n_x = xs_s.shape[0]
-    ahead = 2
+    ahead = 1
+
+    def strip_at(i):
+        return n_x - 2 - 2 * (i // 2) + i % 2
+
     staged = [pltpu.make_async_copy(ref.at[:, c], gb.at[:, n, c], io_sem.at[n])
               for n, ref in enumerate((theta_ref, mom_ref))]
     for cp in staged:
         cp.start()
     for i in range(ahead):
-        x_copy(i).start()
-    local = pltpu.make_async_copy(x_hbm.at[pl.ds(pl.multiple_of(y * rows, rows), rows), :], xv.at[y], loc_sem)
-    local.start()
+        x_copy(strip_at(i)).start()
+    for i in range(n_x):
+        x_local(strip_at(i)).start()
     eb[...] = jnp.broadcast_to(eps_ref[...], (LANES, chains)).T
     for cp in staged:
         cp.wait()
@@ -112,7 +127,7 @@
 
     @pl.loop(ahead, n_x)
     def _(i):
-        x_copy(i).start()
+        x_copy(strip_at(i)).start()
 
     start_copy(1).start()
 
@@ -132,12 +147,10 @@
         gather_mid(j)
     for j in range(nb):
         gather_end(j)
-    local.wait()
-
-    def lhs_of(j, h):
-        top = jnp.concatenate([tb[j, cc, 0, h, xx] for cc in range(2) for xx in range(2)], axis=1)
-        low = jnp.concatenate([tb[j, cc, 1, h, xx] for cc in range(2) for xx in range(2)], axis=1)
-        return jnp.concatenate([top, low], axis=0)
+
+    def lhs_of(j, cc):
+        return jnp.concatenate([jnp.concatenate([tb[j, cc, k, h, xx] for h in range(2) for xx in range(2)], axis=1)
+                                for k in range(2)], axis=0)
 
     def label_row(i, n):
         return lab_ref[:, pl.ds(pl.multiple_of(y * rows + i * n, n), n)].astype(F32)
@@ -146,21 +159,38 @@
         lab = label_row(i, z_rows)
         rt[:, pl.ds(pl.multiple_of(i * z_rows, z_rows), z_rows)] = (lab - jax.nn.sigmoid(z)).astype(BF16)
 
+    def piece(q):
+        return slice(q * z_rows, (q + 1) * z_rows)
+
+    def logits_plain(j, cc, first):
+        left = lhs_of(j, cc)
+        for q in range(n_zc):
+            new = contract_last(left, xa[2 * j + cc, piece(q)])
+            zt[q] = new if first is True else jnp.where(first, 0.0, zt[q]) + new
+
+    def logits_flip(j, cc, end):
+        left = lhs_of(j, cc)
+        for q in range(n_zc):
+            z = zt[q] + jnp.dot(left, xa[nb + 2 * j + cc, piece(q)], preferred_element_type=F32)
+            zt[q] = z
+            if end:
+                residual(q, z)
+
     @pl.loop(0, n_x)
     def _(i):
-        x_copy(i).wait_recv()
-        n = rows // n_x
-        at = pl.ds(pl.multiple_of(i * n, n), n)
-        acc = jnp.zeros((chains, n), F32)
-        for j in range(nb):
-            for h in range(2):
-                acc = acc + contract_last(lhs_of(j, h), xv[h, at, j * wide:(j + 1) * wide])
-        lab = label_row(i, n)
-        rt[:, at] = (lab - jax.nn.sigmoid(acc)).astype(BF16)
-        for j in range(xw.shape[0]):
-            for h in range(2):
-                src = (nb - xw.shape[0] + j) * wide
-                xw[j, h * wide:(h + 1) * wide, at] = xv[h, at, src:src + wide].T
+        u = strip_at(i)
+        j, cc = u // 2, u % 2
+        x_local(u).wait()
+        x_copy(u).wait_recv()
+        logits_plain(j, cc, i == 0)
+
+        @pl.when(j > 0)
+        def _():
+            for q in range(n_zc):
+                xa[nb + u, piece(q)] = xa[u, piece(q)].T
+
+    for q in range(n_zc):
+        residual(q, zt[q])
 
     @pl.loop(0, n_x)
     def _(i):
@@ -168,21 +198,30 @@
 
     start_copy(1).wait()
 
-    def grad_block(j):
-        cols = pl.ds(pl.multiple_of(j * wide, wide), wide)
-        for h in range(2):
-            out = jnp.dot(rt[...], xv[h, :, cols], preferred_element_type=F32)
-            for q in range(4):
-                gb[j, q // 2, h, q % 2] = out[:, q * LANES:(q + 1) * LANES]
+    def grad_half(j, p):
+        if j < nb - 1:
+            out = jnp.dot(rt[...], xa[2 * j + p], preferred_element_type=F32)
+        else:
+            out = contract_last(rt[:, piece(0)], xa[nb + 2 * j + p, piece(0)])
+            for q in range(1, n_zc):
+                out = out + contract_last(rt[:, piece(q)], xa[nb + 2 * j + p, piece(q)])
+        for q in range(4):
+            gb[j, p, q // 2, q % 2] = out[:, q * LANES:(q + 1) * LANES]
+
+    def grad_twin(j, t):
+        grad_half(j, co)
         d2d_copy(j).start()
 
-    def pair_sum(j):
+    def grad_own(j, t):
+        grad_half(j, c)
+
+    def pair_sum(j, t):
         d2d_copy(j).wait()
         gb[j, c] += dd[j]
         for k in range(2):
             rs1_copy(j, k).start()
 
-    def chip_sum(j):
+    def chip_sum(j, t):
         for k in range(2):
             rs1_copy(j, k).wait()
         h2[j, 0] = gb[j, c, :, x, :half] + r1[j, 0]
@@ -209,31 +248,36 @@
             for k in range(2):
                 ag1_copy(j, k).start()
 
-    n_slow = nb - xw.shape[0]
-
-    def logits_block(j):
-        left = [lhs_of(j, h) for h in range(2)]
-
-        @pl.when(j < n_slow)
+        @pl.when(t == LEAPS)
         def _():
-            cols = pl.ds(pl.multiple_of(j * wide, wide), wide)
-
-            @pl.loop(0, n_zc)
-            def _(i):
-                at = pl.ds(pl.multiple_of(i * z_rows, z_rows), z_rows)
-                new = contract_last(left[0], xv[0, at, cols]) + contract_last(left[1], xv[1, at, cols])
-                zt[i] = jnp.where(j == 0, 0.0, zt[i]) + new
-
-        @pl.when(j >= n_slow)
+            last_copy(1, j).start()
+
+    def logits_own(j, t):
+        if j == 0:
+            logits_plain(j, c, True)
+        else:
+            logits_flip(j, c, False)
+
+    def logits_twin(j, t):
+        gather_end(j)
+        if j == 0:
+            logits_plain(j, co, False)
+        else:
+            logits_flip(j, co, j == nb - 1)
+
+    def gather(j, t):
+        gather_mid(j)
+
+    def first_end(j, t):
+        @pl.when(t == LEAPS)
         def _():
-            both = jnp.concatenate(left, axis=1)
-
-            @pl.loop(0, n_zc)
-            def _(i):
-                at = pl.ds(pl.multiple_of(i * z_rows, z_rows), z_rows)
-                zt[i] += jnp.dot(both, xw[j - n_slow, :, at], preferred_element_type=F32)
-
-    d_mid, d_chp, d_upd, d_gat, d_log = 1, 3, 4, 5, 6
+            for i in range(nb):
+                last_copy(0, i).start()
+
+    def add_loss(j, t):
+        @pl.when(t == LEAPS)
+        def _():
+            lsum[...] = lax.fori_loop(0, n_zc, loss, jnp.zeros((chains, LANES), F32))
 
     def loss(i, acc):
         z = zt[i]
@@ -243,49 +287,31 @@
             acc = acc + term[:, q * LANES:(q + 1) * LANES]
         return acc
 
+    stages = {"g": grad_twin, "h": grad_own, "p": pair_sum, "c": chip_sum, "u": update,
+              "m": gather, "o": logits_own, "t": logits_twin, "e": first_end, "l": add_loss}
+    always = "ghpcuel"
+    plan = PLAN
+
     def one_eval(t, carry):
-        steps = jnp.where(t < LEAPS, nb + d_log, nb + d_upd)
-
-        def step(s, carry):
-            def on(delay, fn, *args):
-                @pl.when(jnp.logical_and(s >= delay, s < nb + delay))
-                def _():
-                    fn(s - delay, *args)
-
-            @pl.when(jnp.logical_and(t == LEAPS, s == 0))
-            def _():
-                last_copy(0).start()
-
-            @pl.when(jnp.logical_and(t == LEAPS, s == nb))
-            def _():
-                lsum[...] = lax.fori_loop(0, n_zc, loss, jnp.zeros((chains, LANES), F32))
-
-            on(0, grad_block)
-            on(d_mid, pair_sum)
-            on(d_chp, chip_sum)
-            on(d_upd, update, t)
-
-            @pl.when(t < LEAPS)
-            def _():
-                on(d_gat, gather_mid)
-
-                @pl.when(jnp.logical_and(s >= d_log, s < nb + d_log))
-                def _():
-                    gather_end(s - d_log)
-                    logits_block(s - d_log)
-
-                @pl.when(s == nb + d_log - 1)
-                def _():
-                    @pl.loop(0, n_zc)
-                    def _(i):
-                        residual(i, zt[i])
-            return carry
-
-        return lax.fori_loop(0, steps, step, carry)
+        at = 0
+        while at < len(plan):
+            end = at
+            while end < len(plan) and (plan[end][0] in always) == (plan[at][0] in always):
+                end += 1
+
+            def run(chunk=tuple(plan[at:end])):
+                for op in chunk:
+                    stages[op[0]](int(op[1:] or 0), t)
+
+            if plan[at][0] in always:
+                run()
+            else:
+                pl.when(t < LEAPS)(run)
+            at = end
+        return carry
 
     lax.fori_loop(0, LEAPS + 1, one_eval, 0)
 
-    last_copy(1).start()
     acc = lsum[...]
     for j in range(nb):
         for h in range(2):
@@ -315,9 +341,9 @@
         return remote(gb.at[:, n, c], gb.at[:, n, c], fd_s.at[n], fd_r.at[n], core)
 
     for n in range(2):
-        last_copy(n).wait()
         state = (tf, pf)[n]
         for j in range(nb):
+            last_copy(n, j).wait()
             gb[j, n, c, x] = jnp.concatenate([state[j, 0, y], state[j, 1, x]], axis=0).T
             gb[j, n, c, xo] = jnp.concatenate([xt[n, j], state[j, 1, xo]], axis=0).T
         swap(n).start()
@@ -338,8 +364,8 @@
         rows = n_local // 2
         chains = theta_init.shape[1]
         nb = feats_half // (4 * LANES)
-        z_rows = min(4096, rows)
-        n_x = 16
+        z_rows = min(4 * LANES, rows)
+        n_x = 2 * nb
         tiles = (nb, 2, 2, LANES, chains)
         vm = pl.BlockSpec(memory_space=pltpu.VMEM)
         dma = pltpu.SemaphoreType.DMA
@@ -351,8 +377,7 @@
             in_specs=[far, vm, far, far, vm],
             out_specs=(far, far, vm),
             scratch_shapes=[
-                pltpu.VMEM((2, rows, feats_half), BF16),
-                pltpu.VMEM((nb // 2, 8 * LANES, rows), BF16),
+                pltpu.VMEM((3 * nb, rows, 4 * LANES), BF16),
                 pltpu.VMEM((rows // z_rows, chains, z_rows), F32),
                 pltpu.VMEM((chains, rows), BF16),
                 pltpu.VMEM((nb, 2, 2, 2, chains, LANES), F32),
@@ -367,10 +392,10 @@
                 pltpu.VMEM((chains, LANES), F32),
                 pltpu.VMEM((chains, LANES), F32),
                 pltpu.VMEM((8, 8, chains), F32),
-                dma, dma((4,)), dma((n_x,)), dma((n_x,)), dma((2,)), dma((2,)), dma((nb,)), dma((nb,)),
+                dma((n_x,)), dma((4,)), dma((n_x,)), dma((n_x,)), dma((2,)), dma((2,)), dma((nb,)), dma((nb,)),
                 dma((nb, 2)), dma((nb, 2)), dma((nb, 2)), dma((nb, 2)),
                 dma((nb, 2)), dma((nb, 2)), dma((nb,)), dma((nb,)),
-                dma((2,)), dma((2,)), dma((2,)), dma((2,)), dma((7,)), dma((7,)),
+                dma((2, nb)), dma((2, nb)), dma((2,)), dma((2,)), dma((7,)), dma((7,)),
             ],
             compiler_params=pltpu.CompilerParams(collective_id=0, has_side_effects=True,
                                                  vmem_limit_bytes=67043328),

time: 816 us -> 752 us (0.922)
  Pallas kernels: 809 us -> 745 us
    pallas_call x1, Pallas kernels: 809 us -> 745 us  [local_run(): pl.pallas_call(hmc_kernel, out_shape=(jax.ShapeDtypeStruct(tiles, F32), j...]
where the time goes in v3:
time: 752 us; the launch traced here: 751 us
  Pallas kernels  745 us (99%)
    pallas_call x1, Pallas kernels, local_run(): pl.pallas_call(hmc_kernel, out_shape=(jax.ShapeDtypeStruct(tiles, F32), j...  745 us

profile of v3, /device:TPU:0, one launch (start us, length us, event | category | flops | bytes accessed | tf_op | source)
XLA Modules:
  0.0 751.5 jit_solution(1204992881402645032)
XLA Ops:
  0.6 745.2 %shard_map.76 = (f32[4,2,2,128,128]{4,3,2,1,0:T(8,128)}, f32[4,2,2,128,128]{4,3,2,1,0:T(8,128)}, f32[1,128]{1,0:T(1,128)}) custom-call(bf16[8192,2048]{1,0:T(8,128)(2,1)} %x_hbm.1, s32[1,8192]{1,0:T(1,128)} %bitcast.11, f32[4,2,2,128,128]{4,3,2,1,0:T(8,128)} %bitcast.7, f32[4,2,2,128,128]{4,3,2,1,0:T(8,128)} %bitcast.8, f32[1,128]{1,0:T(1,128)} %bitcast.12), custom_call_target="tpu_custom_call" | custom-call | tf_op jit(solution)/shard_map/pallas_call | solution.py:373
  745.8 2.3 copy.11
  748.1 2.3 copy.12
  750.3 1.1 copy.13

commit v4 on v3

--- a/solution.py
+++ b/solution.py
@@ -13,8 +13,8 @@
 LANES = 128
 PLAN = (
         "e0", "g0", "h0", "g1", "p0", "h1", "g2", "p1", "h2", "p2", "c0", "g3",
-        "c1", "h3", "p3", "l0", "u0", "c2", "c3", "u1", "m0", "o0", "u2", "t0",
-        "u3", "m1", "o1", "m2", "o2", "t1", "m3", "o3", "t2", "t3",
+        "c1", "h3", "p3", "l0", "s0", "u0", "c2", "c3", "u1", "m0", "o0", "u2",
+        "t0", "u3", "m1", "o1", "m2", "o2", "t1", "m3", "o3", "t2", "t3",
 )
 F32 = jnp.float32
 BF16 = jnp.bfloat16
@@ -25,9 +25,9 @@
 
 
 def hmc_kernel(x_hbm, lab_ref, theta_ref, mom_ref, eps_ref,
-               th_out, mo_out, en_out,
+               st_out, en_out,
                xa, zt, rt, gb, dd, r1, h2, r2, tb, tf, pf, xt, eb, lsum, ebuf,
-               loc_sem, io_sem, xs_s, xs_r, in_s, in_r, ds_s, ds_r, r1_s, r1_r, r2_s, r2_r, a1_s, a1_r, ad_s, ad_r,
+               loc_sem, io_sem, xs_s, xs_r, in_s, in_r, sd_s, sd_r, ds_s, ds_r, r1_s, r1_r, r2_s, r2_r, a1_s, a1_r, ad_s, ad_r,
                fx_s, fx_r, fd_s, fd_r, en_s, en_r):
     nb = tb.shape[0]
     chains = zt.shape[1]
@@ -64,12 +64,19 @@
         pl.semaphore_signal(barrier, inc=1, device_id=dev, device_id_type=MESH)
     pl.semaphore_wait(barrier, 7)
 
-    def strip_refs(u, here):
-        src = x_hbm.at[pl.ds(pl.multiple_of(here * rows, rows), rows), pl.ds(pl.multiple_of(u * strip, strip), strip)]
-        return src, xa.at[u, :, pl.ds(pl.multiple_of(y * strip, strip), strip)]
+    def strip_refs(u, here, at=0, n=rows):
+        src = x_hbm.at[pl.ds(pl.multiple_of(here * rows + at, n), n), pl.ds(pl.multiple_of(u * strip, strip), strip)]
+        return src, xa.at[u, at:at + n, pl.ds(pl.multiple_of(y * strip, strip), strip)]
 
     def x_copy(u):
         return remote(*strip_refs(u, yo), xs_s.at[u], xs_r.at[u], y_nbr)
+
+    parts = 4
+
+    def x_last(k):
+        n = rows // parts
+        sem = 1 if k == 0 else n_x + k - 1
+        return remote(*strip_refs(1, yo, k * n, n), xs_s.at[sem], xs_r.at[sem], y_nbr)
 
     def x_local(u):
         return pltpu.make_async_copy(*strip_refs(u, y), loc_sem.at[u])
@@ -87,6 +94,10 @@
     def ag1_copy(j, k):
         ref = (tb.at[j, c, 0, :, x], tb.at[j, c, 1, y])[k]
         return remote(ref, ref, a1_s.at[j, k], a1_r.at[j, k], pair[k])
+
+    def seed_copy(n):
+        ref = (tb.at[:, c, :, y, x], tb.at[:, c, :, :, x])[n]
+        return remote(ref, ref, sd_s.at[n], sd_r.at[n], pair[1 - n])
 
     def start_copy(n):
         ref = (tf, pf)[n].at[:, 0, y]
@@ -118,18 +129,21 @@
         for xx in range(2):
             tf[j, 1, xx] = gb[j, 0, c, xx].T[half:]
             pf[j, 1, xx] = gb[j, 1, c, xx].T[half:]
-            tb[j, c, 1, y, xx] = tf[j, 1, xx].astype(BF16)
         tf[j, 0, y] = gb[j, 0, c, x].T[:half]
         pf[j, 0, y] = gb[j, 1, c, x].T[:half]
-    start_copy(0).start()
-    for j in range(nb):
-        ag1_copy(j, 1).start()
-
-    @pl.loop(ahead, n_x)
+        tb[j, c, 0, y, x] = tf[j, 0, y].astype(BF16)
+        tb[j, c, 1, y, x] = tf[j, 1, x].astype(BF16)
+    seed_copy(0).start()
+
+    @pl.loop(ahead, n_x - 1)
     def _(i):
         x_copy(strip_at(i)).start()
 
-    start_copy(1).start()
+    for k in range(parts):
+        x_last(k).start()
+
+    for n in range(2):
+        start_copy(n).start()
 
     def gather_mid(j):
         for k in range(2):
@@ -139,12 +153,12 @@
     def gather_end(j):
         agd_copy(j).wait()
 
-    start_copy(0).wait()
+    for n in range(2):
+        seed_copy(n).wait()
+        if n == 0:
+            seed_copy(1).start()
     for j in range(nb):
-        tb[j, c, 0, :, x] = tf[j, 0].astype(BF16)
-        ag1_copy(j, 0).start()
-    for j in range(nb):
-        gather_mid(j)
+        agd_copy(j).start()
     for j in range(nb):
         gather_end(j)
 
@@ -176,7 +190,7 @@
             if end:
                 residual(q, z)
 
-    @pl.loop(0, n_x)
+    @pl.loop(0, n_x - 1)
     def _(i):
         u = strip_at(i)
         j, cc = u // 2, u % 2
@@ -189,14 +203,20 @@
             for q in range(n_zc):
                 xa[nb + u, piece(q)] = xa[u, piece(q)].T
 
-    for q in range(n_zc):
-        residual(q, zt[q])
-
-    @pl.loop(0, n_x)
+    x_local(1).wait()
+    left = lhs_of(0, 1)
+    for k in range(parts):
+        x_last(k).wait_recv()
+        for q in range(k * n_zc // parts, (k + 1) * n_zc // parts):
+            residual(q, zt[q] + contract_last(left, xa[1, piece(q)]))
+
+    @pl.loop(0, n_x - 1)
     def _(i):
-        x_copy(i).wait_send()
-
-    start_copy(1).wait()
+        x_copy(strip_at(i)).wait_send()
+
+    for k in range(parts):
+        x_last(k).wait_send()
+
 
     def grad_half(j, p):
         if j < nb - 1:
@@ -268,6 +288,12 @@
     def gather(j, t):
         gather_mid(j)
 
+    def start_end(j, t):
+        @pl.when(t == 0)
+        def _():
+            for n in range(2):
+                start_copy(n).wait()
+
     def first_end(j, t):
         @pl.when(t == LEAPS)
         def _():
@@ -288,8 +314,8 @@
         return acc
 
     stages = {"g": grad_twin, "h": grad_own, "p": pair_sum, "c": chip_sum, "u": update,
-              "m": gather, "o": logits_own, "t": logits_twin, "e": first_end, "l": add_loss}
-    always = "ghpcuel"
+              "m": gather, "o": logits_own, "t": logits_twin, "e": first_end, "l": add_loss, "s": start_end}
+    always = set("ghpcuels")
     plan = PLAN
 
     def one_eval(t, carry):
@@ -335,7 +361,7 @@
 
     def put(n, k):
         cc = (c, co)[k]
-        return pltpu.make_async_copy(gb.at[:, n, cc], (th_out, mo_out)[n].at[:, cc], io_sem.at[2 * k + n])
+        return pltpu.make_async_copy(gb.at[:, n, cc], st_out.at[n, :, cc], io_sem.at[2 * k + n])
 
     def swap(n):
         return remote(gb.at[:, n, c], gb.at[:, n, c], fd_s.at[n], fd_r.at[n], core)
@@ -370,12 +396,11 @@
         vm = pl.BlockSpec(memory_space=pltpu.VMEM)
         dma = pltpu.SemaphoreType.DMA
         far = pl.BlockSpec(memory_space=pl.ANY)
-        th, mo, en = pl.pallas_call(
+        state, en = pl.pallas_call(
             hmc_kernel,
-            out_shape=(jax.ShapeDtypeStruct(tiles, F32), jax.ShapeDtypeStruct(tiles, F32),
-                       jax.ShapeDtypeStruct((1, chains), F32)),
+            out_shape=(jax.ShapeDtypeStruct((2,) + tiles, F32), jax.ShapeDtypeStruct((1, chains), F32)),
             in_specs=[far, vm, far, far, vm],
-            out_specs=(far, far, vm),
+            out_specs=(far, vm),
             scratch_shapes=[
                 pltpu.VMEM((3 * nb, rows, 4 * LANES), BF16),
                 pltpu.VMEM((rows // z_rows, chains, z_rows), F32),
@@ -392,7 +417,7 @@
                 pltpu.VMEM((chains, LANES), F32),
                 pltpu.VMEM((chains, LANES), F32),
                 pltpu.VMEM((8, 8, chains), F32),
-                dma((n_x,)), dma((4,)), dma((n_x,)), dma((n_x,)), dma((2,)), dma((2,)), dma((nb,)), dma((nb,)),
+                dma((n_x,)), dma((4,)), dma((n_x + 3,)), dma((n_x + 3,)), dma((2,)), dma((2,)), dma((2,)), dma((2,)), dma((nb,)), dma((nb,)),
                 dma((nb, 2)), dma((nb, 2)), dma((nb, 2)), dma((nb, 2)),
                 dma((nb, 2)), dma((nb, 2)), dma((nb,)), dma((nb,)),
                 dma((2, nb)), dma((2, nb)), dma((2,)), dma((2,)), dma((7,)), dma((7,)),
@@ -401,7 +426,7 @@
                                                  vmem_limit_bytes=67043328),
         )(x_local, labels[None, :], theta_init.reshape(tiles), mom_init.reshape(tiles),
           step_size[None, :])
-        return th.reshape(theta_init.shape), mo.reshape(theta_init.shape), en.reshape(chains)
+        return state[0].reshape(theta_init.shape), state[1].reshape(theta_init.shape), en.reshape(chains)
 
     return jax.shard_map(local_run, mesh=mesh,
                          in_specs=(P("data", "feat"), P("data"), chain_spec, chain_spec, P("parts")),

time: 752 us -> 745 us (level)
  no operation moved by 1% of the time
where the time goes in v4:
time: 745 us
  Pallas kernels  741 us (99%)
    pallas_call x1, Pallas kernels, local_run(): pl.pallas_call(hmc_kernel, out_shape=(jax.ShapeDtypeStruct((2,) + tiles,...  741 us

profile of v4, /device:TPU:0, one launch (start us, length us, event | category | flops | bytes accessed | tf_op | source)
XLA Modules:
  0.0 745.3 jit_solution(11423458018341228130)
XLA Ops:
  0.6 741.0 %shard_map.76 = (f32[2,4,2,2,128,128]{5,4,3,2,1,0:T(8,128)}, f32[1,128]{1,0:T(1,128)}) custom-call(bf16[8192,2048]{1,0:T(8,128)(2,1)} %x_hbm.1, s32[1,8192]{1,0:T(1,128)} %bitcast.11, f32[4,2,2,128,128]{4,3,2,1,0:T(8,128)} %bitcast.7, f32[4,2,2,128,128]{4,3,2,1,0:T(8,128)} %bitcast.8, f32[1,128]{1,0:T(1,128)} %bitcast.12), custom_call_target="tpu_custom_call" | custom-call | tf_op jit(solution)/shard_map/pallas_call | solution.py:399
  741.7 0.0 copy-start
  741.7 3.1 fusion
  744.8 0.0 copy-done
  744.8 0.5 copy.9
Async XLA Ops:
  741.7 3.1 copy-start

commit v5 on v4

--- a/solution.py
+++ b/solution.py
@@ -12,9 +12,9 @@
 MESH = pl.DeviceIdType.MESH
 LANES = 128
 PLAN = (
-        "e0", "g0", "h0", "g1", "p0", "h1", "g2", "p1", "h2", "p2", "c0", "g3",
-        "c1", "h3", "p3", "l0", "s0", "u0", "c2", "c3", "u1", "m0", "o0", "u2",
-        "t0", "u3", "m1", "o1", "m2", "o2", "t1", "m3", "o3", "t2", "t3",
+        "e0", "g1", "h0", "p0", "h1", "g2", "p1", "h2", "p2", "c0", "g3", "c1",
+        "h3", "p3", "l0", "s0", "u0", "c2", "c3", "u1", "m0", "o0", "u2", "t0",
+        "u3", "m1", "o1", "m2", "o2", "t1", "m3", "o3", "t2", "t3", "n0",
 )
 F32 = jnp.float32
 BF16 = jnp.bfloat16
@@ -314,7 +314,7 @@
         return acc
 
     stages = {"g": grad_twin, "h": grad_own, "p": pair_sum, "c": chip_sum, "u": update,
-              "m": gather, "o": logits_own, "t": logits_twin, "e": first_end, "l": add_loss, "s": start_end}
+              "m": gather, "o": logits_own, "t": logits_twin, "n": grad_twin, "e": first_end, "l": add_loss, "s": start_end}
     always = set("ghpcuels")
     plan = PLAN
 
@@ -336,6 +336,7 @@
             at = end
         return carry
 
+    grad_twin(0, 0)
     lax.fori_loop(0, LEAPS + 1, one_eval, 0)
 
     acc = lsum[...]

time: 745 us -> 743 us (level)
  no operation moved by 1% of the time
where the time goes in v5:
time: 743 us
  Pallas kernels  739 us (99%)
    pallas_call x1, Pallas kernels, local_run(): pl.pallas_call(hmc_kernel, out_shape=(jax.ShapeDtypeStruct((2,) + tiles,...  739 us

profile of v5, /device:TPU:0, one launch (start us, length us, event | category | flops | bytes accessed | tf_op | source)
XLA Modules:
  0.0 742.8 jit_solution(15025831295646663108)
XLA Ops:
  0.6 738.5 %shard_map.76 = (f32[2,4,2,2,128,128]{5,4,3,2,1,0:T(8,128)}, f32[1,128]{1,0:T(1,128)}) custom-call(bf16[8192,2048]{1,0:T(8,128)(2,1)} %x_hbm.1, s32[1,8192]{1,0:T(1,128)} %bitcast.11, f32[4,2,2,128,128]{4,3,2,1,0:T(8,128)} %bitcast.7, f32[4,2,2,128,128]{4,3,2,1,0:T(8,128)} %bitcast.8, f32[1,128]{1,0:T(1,128)} %bitcast.12), custom_call_target="tpu_custom_call" | custom-call | tf_op jit(solution)/shard_map/pallas_call | solution.py:400
  739.1 0.0 copy-start
  739.2 3.1 fusion
  742.2 0.0 copy-done
  742.2 0.5 copy.9
Async XLA Ops:
  739.1 3.1 copy-start
